TPU v7x, 256 devices: a whole 4x4x8 slice. The times are simulated.
256 devices in a mesh: gx: 32 (over y, z), gy: 8 (over x, core).
Axes of the slice: x: 4, y: 4, z: 8, core: 2. Of those that a mesh axis runs over, the one named last changes fastest.
Arguments:
- right_side: float32 [64, 128, 4, 3, 128], P('gx', 'gy'), may hold values from -6 to 6
- stencil: float32 [27, 3, 3], replicated, as said below
- class_scale: float32 [8], replicated, may hold values from 0.5 to 4
- material: int32 [64, 128, 128], P('gx', 'gy'), may hold values from 0 to 7
- boundary: int32 [64, 128, 128], P('gx', 'gy'), may hold values 0 or 1
- sign_bits: int32 [64, 128, 3, 128], P('gx', 'gy'), may hold values from 0 to 1
- sample_rows: int32 [32, 8, 128], P('gx', 'gy'), may hold values from 0 to 12287
Outputs:
- solution: float32 [64, 128, 4, 3, 128], P('gx', 'gy')
- residual: float32 [64, 128, 4, 3, 128], P('gx', 'gy')
Inputs may be any that keep to these rules, and one draw needn't show every extreme that they name: In every row of the centre block stencil[13], the diagonal entry exceeds the sum of the magnitudes of all other entries of that row over all 27 blocks.
All inputs are finite; a program needn't handle non-finite values. No bound on the sum of `boundary` on one device may be relied on, other than what follows from the above.
Results may differ from a plain program's by a relative error of at most 0.0028.
Values sent between devices are 32-bit elements; how exact they have to be, the bound alone decides.
No kernel may reach another device: no remote copies, remote signals or barrier semaphores. Data moves between devices by JAX's collectives and lax.ppermute only.
A program may use at most 64 MiB of HBM per device.

v0:
```python
import math
import jax
import jax.numpy as jnp
from jax import lax
from jax.sharding import Mesh
from jax.sharding import PartitionSpec as P

STEPS = 8
GX_GY = ("gx_0", "gx_1", "gy_0", "gy_1")
GX = ("gx_0", "gx_1")
GY = ("gy_0", "gy_1")
exact_mode = lax.Precision.HIGHEST


def padded_2(cells, sides, width):
    for axis, dim in sides:
        count = lax.axis_size(axis)
        ends = count - 1
        head = lax.slice_in_dim(cells, 0, width, axis=dim)
        tail = lax.slice_in_dim(cells, cells.shape[dim] - width, cells.shape[dim], axis=dim)
        cells = jnp.concatenate(
            [
                lax.ppermute(tail, axis, [(i, (i + 1) % count) for i in range(ends)]),
                cells,
                lax.ppermute(head, axis, [((i + 1) % count, i) for i in range(ends)]),
            ],
            axis=dim,
        )
    return cells


def one_axis_at_a_time(shard, axes):
    for axis in axes:
        shard = lax.psum(shard, axis)
    return shard


def hadamard_table():
    lanes = jnp.arange(128, dtype=jnp.int32)
    common = lanes[:, None] & lanes[None, :]
    parity = jnp.zeros((128, 128), jnp.int32)
    for bit in range(7):
        parity = parity + (common >> bit & 1)
    return (1 - 2 * (parity % 2)).astype(jnp.float32) / math.sqrt(128.0)


def material_scale(material, class_scale):
    scale_field = jnp.zeros(material.shape, jnp.float32)
    for number in range(class_scale.shape[0]):
        scale_field = scale_field + jnp.where(
            material == number, class_scale[number], jnp.float32(0.0)
        )
    return scale_field


def extend(field):
    return padded_2(field, ((GX, 0), (GY, 1)), 1)


def operate(field, stencil, scale_field, boundary):
    padded = jnp.pad(extend(field), ((0, 0), (0, 0), (0, 0), (0, 0), (1, 1)))
    extent_x, extent_y, extent_z = (field.shape[0], field.shape[1], field.shape[4])
    summed = jnp.zeros(field.shape, jnp.float32)
    for offset_x in range(3):
        for offset_y in range(3):
            for offset_z in range(3):
                shifted = padded[
                    offset_x : offset_x + extent_x,
                    offset_y : offset_y + extent_y,
                    :,
                    :,
                    offset_z : offset_z + extent_z,
                ]
                coupling = stencil[offset_x * 9 + offset_y * 3 + offset_z]
                summed = summed + jnp.sum(
                    coupling[:, :, None] * shifted[:, :, :, None, :, :], axis=4
                )
    return jnp.where(
        boundary[:, :, None, None, :] == 1, field, scale_field[:, :, None, None, :] * summed
    )


def sketch_local(field, sign_field, picks, table):
    pick_x, pick_y, pick_comp, pick_block, pick_lane = picks
    signed = field * sign_field[:, :, None, :, :]
    tiled = signed.reshape(field.shape[:4] + (field.shape[4] // 128, 128))
    chosen = tiled[pick_x, pick_y, :, pick_comp, pick_block]
    return jnp.sum(chosen * table[pick_lane][:, None, :], axis=-1)


def back_substitute(triangle, projected):
    count = triangle.shape[0]

    def one_row(step, unknowns):
        row = count - 1 - step
        line = triangle[row]
        total = jnp.dot(line[None, :], unknowns, precision=exact_mode)[0]
        value = (projected[row] - total) / line[row]
        return unknowns.at[row].set(value)

    return lax.fori_loop(0, count, one_row, jnp.zeros(projected.shape, jnp.float32))


def solve_small(matrix, rhs):
    count = matrix.shape[1]
    columns = matrix.T

    def one_column(column, state_pair):
        orthonormal, triangle = state_pair
        vector = columns[column]
        first_pass = jnp.dot(orthonormal.T, vector, precision=exact_mode)
        vector = vector - jnp.dot(orthonormal, first_pass, precision=exact_mode)
        second_pass = jnp.dot(orthonormal.T, vector, precision=exact_mode)
        vector = vector - jnp.dot(orthonormal, second_pass, precision=exact_mode)
        length = jnp.sqrt(jnp.sum(vector * vector) + 1e-06)
        orthonormal = orthonormal.at[:, column].set(vector / length)
        triangle = triangle.at[:, column].set((first_pass + second_pass).at[column].set(length))
        return (orthonormal, triangle)

    start = (jnp.zeros(matrix.shape, jnp.float32), jnp.zeros((count, count), jnp.float32))
    orthonormal, triangle = lax.fori_loop(0, count, one_column, start)
    projected = jnp.dot(orthonormal.T, rhs, precision=exact_mode)
    return back_substitute(triangle, projected)


def shards(right_side, stencil, class_scale, material, boundary, sign_bits, sample_rows):
    table = hadamard_table()
    scale_field = material_scale(material, class_scale)
    sign_field = (2 * sign_bits - 1).astype(jnp.float32)
    depth = right_side.shape[4]
    plane = right_side.shape[1] * 3 * depth
    sampled = sample_rows[0, 0]
    rest_y = sampled % plane
    rest_c = rest_y % (3 * depth)
    pick_z = rest_c % depth
    picks = (sampled // plane, rest_y // (3 * depth), rest_c // depth, pick_z // 128, pick_z % 128)
    width = right_side.shape[2]
    local_rhs = sketch_local(right_side, sign_field, picks, table)
    sketch_rhs = one_axis_at_a_time(local_rhs, GX_GY)
    lengths = jnp.sqrt(jnp.sum(sketch_rhs * sketch_rhs, axis=0) + 1e-06)
    basis_block = right_side / lengths[None, None, :, None, None]
    sketch_basis = sketch_rhs / lengths
    blocks = []
    sketched_images = []
    for block_step in range(STEPS):
        operated = operate(basis_block, stencil, scale_field, boundary)
        local_image = sketch_local(operated, sign_field, picks, table)
        sketch_image = one_axis_at_a_time(local_image, GX_GY)
        blocks.append(basis_block)
        sketched_images.append(sketch_image)
        if block_step + 1 < STEPS:
            coupling = jnp.dot(sketch_basis.T, sketch_image, precision=exact_mode)
            remainder = operated - jnp.einsum(
                "xyicz,ij->xyjcz", basis_block, coupling, precision=exact_mode
            )
            sketch_remainder = sketch_image - jnp.dot(sketch_basis, coupling, precision=exact_mode)
            norms = jnp.sqrt(jnp.sum(sketch_remainder * sketch_remainder, axis=0) + 1e-06)
            basis_block = remainder / norms[None, None, :, None, None]
            sketch_basis = sketch_remainder / norms
    matrix = jnp.concatenate(sketched_images, axis=1)
    weights = solve_small(matrix, sketch_rhs)
    solution = jnp.zeros(right_side.shape, jnp.float32)
    for block_step in range(STEPS):
        part_weights = weights[block_step * width : (block_step + 1) * width]
        solution = solution + jnp.einsum(
            "xyicz,ij->xyjcz", blocks[block_step], part_weights, precision=exact_mode
        )
    residual = right_side - operate(solution, stencil, scale_field, boundary)
    return (solution, residual)


def solution(mesh):
    split = Mesh(mesh.devices.reshape(4, 8, 4, 2), ("gx_0", "gx_1", "gy_0", "gy_1"))
    return jax.shard_map(
        shards,
        mesh=split,
        in_specs=(
            P(GX, GY, None, None, None),
            P(),
            P(),
            P(GX, GY, None),
            P(GX, GY, None),
            P(GX, GY, None, None),
            P(GX, GY, None),
        ),
        out_specs=(P(GX, GY, None, None, None), P(GX, GY, None, None, None)),
        check_vma=False,
    )
```

profile of v0, /device:TPU:10, one launch (start us, length us, event | category | flops | bytes accessed | tf_op | source)
XLA Modules:
  0.0 823.2 jit_solution(13014205767853807181)
XLA Ops:
  6.1 8.7 %psum.252 = f32[128,4]{0,1:T(4,128)S(1)} all-reduce(f32[128,4]{0,1:T(4,128)S(1)} %copy.1897), channel_id=1, replica_groups=mesh['gx_0'=4,'gx_1'=8,'gy_0'=4,'gy_1'=2] {'gx_0'}, use_global_device_ids=true, to_apply=%region_1.2 | all-reduce | flops 512 | bytes 4096 | tf_op jit(solution)/shard_map/psum | solution.py:34
  14.8 20.0 %psum.253 = f32[128,4]{0,1:T(4,128)S(1)} all-reduce(f32[128,4]{0,1:T(4,128)S(1)} %psum.252), channel_id=1, replica_groups=mesh['gx_0'=4,'gx_1'=8,'gy_0'=4,'gy_1'=2] {'gx_1'}, use_global_device_ids=true, to_apply=%region_2.3 | all-reduce | flops 512 | bytes 4096 | tf_op jit(solution)/shard_map/psum | solution.py:34
  34.7 8.6 %psum.254 = f32[128,4]{0,1:T(4,128)S(1)} all-reduce(f32[128,4]{0,1:T(4,128)S(1)} %psum.253), channel_id=1, replica_groups=mesh['gx_0'=4,'gx_1'=8,'gy_0'=4,'gy_1'=2] {'gy_0'}, use_global_device_ids=true, to_apply=%region_3.4 | all-reduce | flops 512 | bytes 4096 | tf_op jit(solution)/shard_map/psum | solution.py:34
  72.6 10.2 %psum.256 = f32[128,4]{0,1:T(4,128)S(1)} all-reduce(f32[128,4]{0,1:T(4,128)S(1)} %copy.1900), channel_id=1, replica_groups=mesh['gx_0'=4,'gx_1'=8,'gy_0'=4,'gy_1'=2] {'gx_0'}, use_global_device_ids=true, to_apply=%region_34.35 | all-reduce | flops 512 | bytes 4096 | tf_op jit(solution)/shard_map/psum | solution.py:34
  82.8 16.0 %psum.257 = f32[128,4]{0,1:T(4,128)S(1)} all-reduce(f32[128,4]{0,1:T(4,128)S(1)} %psum.256), channel_id=1, replica_groups=mesh['gx_0'=4,'gx_1'=8,'gy_0'=4,'gy_1'=2] {'gx_1'}, use_global_device_ids=true, to_apply=%region_35.36 | all-reduce | flops 512 | bytes 4096 | tf_op jit(solution)/shard_map/psum | solution.py:34
  98.9 6.7 psum.258
  135.2 7.9 psum.260
  143.1 14.1 %psum.261 = f32[128,4]{0,1:T(4,128)S(1)} all-reduce(f32[128,4]{0,1:T(4,128)S(1)} %psum.260), channel_id=1, replica_groups=mesh['gx_0'=4,'gx_1'=8,'gy_0'=4,'gy_1'=2] {'gx_1'}, use_global_device_ids=true, to_apply=%region_68.69 | all-reduce | flops 512 | bytes 4096 | tf_op jit(solution)/shard_map/psum | solution.py:34
  157.2 7.5 psum.262
  196.0 7.3 psum.264
  203.3 15.0 %psum.265 = f32[128,4]{0,1:T(4,128)S(1)} all-reduce(f32[128,4]{0,1:T(4,128)S(1)} %psum.264), channel_id=1, replica_groups=mesh['gx_0'=4,'gx_1'=8,'gy_0'=4,'gy_1'=2] {'gx_1'}, use_global_device_ids=true, to_apply=%region_101.102 | all-reduce | flops 512 | bytes 4096 | tf_op jit(solution)/shard_map/psum | solution.py:34
  218.3 7.3 psum.266
  256.8 6.7 psum.268
  263.5 15.6 %psum.269 = f32[128,4]{0,1:T(4,128)S(1)} all-reduce(f32[128,4]{0,1:T(4,128)S(1)} %psum.268), channel_id=1, replica_groups=mesh['gx_0'=4,'gx_1'=8,'gy_0'=4,'gy_1'=2] {'gx_1'}, use_global_device_ids=true, to_apply=%region_134.135 | all-reduce | flops 512 | bytes 4096 | tf_op jit(solution)/shard_map/psum | solution.py:34
  279.1 7.3 psum.270
  317.6 6.5 psum.272
  324.2 15.8 %psum.273 = f32[128,4]{0,1:T(4,128)S(1)} all-reduce(f32[128,4]{0,1:T(4,128)S(1)} %psum.272), channel_id=1, replica_groups=mesh['gx_0'=4,'gx_1'=8,'gy_0'=4,'gy_1'=2] {'gx_1'}, use_global_device_ids=true, to_apply=%region_167.168 | all-reduce | flops 512 | bytes 4096 | tf_op jit(solution)/shard_map/psum | solution.py:34
  339.9 7.3 psum.274
  378.4 6.5 psum.276
  385.0 15.8 %psum.277 = f32[128,4]{0,1:T(4,128)S(1)} all-reduce(f32[128,4]{0,1:T(4,128)S(1)} %psum.276), channel_id=1, replica_groups=mesh['gx_0'=4,'gx_1'=8,'gy_0'=4,'gy_1'=2] {'gx_1'}, use_global_device_ids=true, to_apply=%region_200.201 | all-reduce | flops 512 | bytes 4096 | tf_op jit(solution)/shard_map/psum | solution.py:34
  400.7 7.3 psum.278
  419.3 6.3 collective-permute-done.24
  439.2 6.5 psum.280
  445.7 15.8 %psum.281 = f32[128,4]{0,1:T(4,128)S(1)} all-reduce(f32[128,4]{0,1:T(4,128)S(1)} %psum.280), channel_id=1, replica_groups=mesh['gx_0'=4,'gx_1'=8,'gy_0'=4,'gy_1'=2] {'gx_1'}, use_global_device_ids=true, to_apply=%region_233.234 | all-reduce | flops 512 | bytes 4096 | tf_op jit(solution)/shard_map/psum | solution.py:34
  461.5 7.3 psum.282
  480.0 6.3 collective-permute-done.28
  500.0 6.5 psum.284
  506.5 15.8 %psum.285 = f32[128,4]{0,1:T(4,128)S(1)} all-reduce(f32[128,4]{0,1:T(4,128)S(1)} %psum.284), channel_id=1, replica_groups=mesh['gx_0'=4,'gx_1'=8,'gy_0'=4,'gy_1'=2] {'gx_1'}, use_global_device_ids=true, to_apply=%region_266.267 | all-reduce | flops 512 | bytes 4096 | tf_op jit(solution)/shard_map/psum | solution.py:34
  522.3 7.3 psum.286
  532.1 173.4 %while.35 = (s32[]{:T(128)}, f32[128,32]{0,1:T(8,128)S(1)}, f32[32,32]{0,1:T(8,128)S(1)}, f32[32,128]{1,0:T(8,128)S(1)}, s32[]{:T(128)}, /*index=5*/s32[1]{0:T(128)}, f32[]{:T(128)}, s32[]{:T(128)}, s32[1]{0:T(128)}) while((s32[]{:T(128)}, f32[128,32]{0,1:T(8,128)S(1)}, f32[32,32]{0,1:T(8,128)S(1)}, f32[32,128]{1,0:T(8,128)S(1)}, ...), condition=%wide.region_272.273_spmd, body=%wide.region_269.272_spmd.sunk | while | flops 197457 | bytes 72798 | solution.py:121
  705.6 85.4 %while.36 = (s32[]{:T(128)}, f32[32,4]{1,0:T(8,128)S(1)}, f32[32,4]{1,0:T(8,128)S(1)}, f32[32,32]{1,0:T(8,128)S(1)}, s32[]{:T(128)}, /*index=5*/s32[2]{0:T(128)S(1)}, s32[1]{0:T(128)}, s32[]{:T(128)}, s32[]{:T(128)}, s32[]{:T(128)}) while((s32[]{:T(128)}, f32[32,4]{1,0:T(8,128)S(1)}, f32[32,4]{1,0:T(8,128)S(1)}, ...), condition=%wide.region_275.276_spmd, body=%wide.region_273.275_spmd.sunk | while | flops 1564 | bytes 20220 | solution.py:101
  803.7 6.3 collective-permute-done.32
  (985 shorter events, 479.6 us)
Async XLA Ops:
  46.0 12.2 %collective-permute-start.1 = (f32[1,16,4,3,128]{4,1,3,2,0:T(8,128)S(1)}, f32[1,16,4,3,128]{4,1,3,2,0:T(8,128)S(1)}, u32[]{:S(2)}, u32[]{:S(2)}) collective-permute-start(f32[1,16,4,3,128]{4,1,3,2,0:T(8,128)S(1)} %get-tuple-element.683), channel_id=1, source_target_pairs={{8,0},{16,8},{24,16},{32,24},{40,32},{48,40},{56,48},{64,56},{72,6... | collective-permute-start | bytes 294920 | tf_op jit(solution)/shard_map/ppermute | solution.py:25
  49.7 8.6 %collective-permute-start = (f32[1,16,4,3,128]{4,1,3,2,0:T(8,128)S(1)}, f32[1,16,4,3,128]{4,1,3,2,0:T(8,128)S(1)}, u32[]{:S(2)}, u32[]{:S(2)}) collective-permute-start(f32[1,16,4,3,128]{4,1,3,2,0:T(8,128)S(1)} %get-tuple-element.682), channel_id=1, source_target_pairs={{0,8},{8,16},{16,24},{24,32},{32,40},{40,48},{48,56},{56,64},{64,7... | collective-permute-start | bytes 294920 | tf_op jit(solution)/shard_map/ppermute | solution.py:23
  58.4 5.5 collective-permute-start.3
  61.9 5.1 collective-permute-start.2
  109.3 6.8 collective-permute-start.5
  111.2 8.9 %collective-permute-start.4 = (f32[1,16,4,3,128]{4,1,3,2,0:T(8,128)S(1)}, f32[1,16,4,3,128]{4,1,3,2,0:T(8,128)S(1)}, u32[]{:S(2)}, u32[]{:S(2)}) collective-permute-start(f32[1,16,4,3,128]{4,1,3,2,0:T(8,128)S(1)} %get-tuple-element.678), channel_id=1, source_target_pairs={{0,8},{8,16},{16,24},{24,32},{32,40},{40,48},{48,56},{56,64},{64,7... | collective-permute-start | bytes 294920 | tf_op jit(solution)/shard_map/ppermute | solution.py:23
  120.1 6.2 collective-permute-start.7
  124.0 5.1 collective-permute-start.6
  168.4 7.0 collective-permute-start.9
  173.1 8.6 %collective-permute-start.8 = (f32[1,16,4,3,128]{4,1,3,2,0:T(8,128)S(1)}, f32[1,16,4,3,128]{4,1,3,2,0:T(8,128)S(1)}, u32[]{:S(2)}, u32[]{:S(2)}) collective-permute-start(f32[1,16,4,3,128]{4,1,3,2,0:T(8,128)S(1)} %get-tuple-element.674), channel_id=1, source_target_pairs={{0,8},{8,16},{16,24},{24,32},{32,40},{40,48},{48,56},{56,64},{64,7... | collective-permute-start | bytes 294920 | tf_op jit(solution)/shard_map/ppermute | solution.py:23
  181.8 5.2 collective-permute-start.11
  184.8 5.2 collective-permute-start.10
  229.3 7.6 collective-permute-start.13
  234.5 8.6 %collective-permute-start.12 = (f32[1,16,4,3,128]{4,1,3,2,0:T(8,128)S(1)}, f32[1,16,4,3,128]{4,1,3,2,0:T(8,128)S(1)}, u32[]{:S(2)}, u32[]{:S(2)}) collective-permute-start(f32[1,16,4,3,128]{4,1,3,2,0:T(8,128)S(1)} %get-tuple-element.670), channel_id=1, source_target_pairs={{0,8},{8,16},{16,24},{24,32},{32,40},{40,48},{48,56},{56,64},{64,7... | collective-permute-start | bytes 294920 | tf_op jit(solution)/shard_map/ppermute | solution.py:23
  243.1 4.9 collective-permute-start.15
  245.6 5.2 collective-permute-start.14
  290.1 7.6 collective-permute-start.17
  295.3 8.6 %collective-permute-start.16 = (f32[1,16,4,3,128]{4,1,3,2,0:T(8,128)S(1)}, f32[1,16,4,3,128]{4,1,3,2,0:T(8,128)S(1)}, u32[]{:S(2)}, u32[]{:S(2)}) collective-permute-start(f32[1,16,4,3,128]{4,1,3,2,0:T(8,128)S(1)} %get-tuple-element.666), channel_id=1, source_target_pairs={{0,8},{8,16},{16,24},{24,32},{32,40},{40,48},{48,56},{56,64},{64,7... | collective-permute-start | bytes 294920 | tf_op jit(solution)/shard_map/ppermute | solution.py:23
  306.4 5.2 collective-permute-start.18
  350.9 7.6 collective-permute-start.21
  356.1 8.6 %collective-permute-start.20 = (f32[1,16,4,3,128]{4,1,3,2,0:T(8,128)S(1)}, f32[1,16,4,3,128]{4,1,3,2,0:T(8,128)S(1)}, u32[]{:S(2)}, u32[]{:S(2)}) collective-permute-start(f32[1,16,4,3,128]{4,1,3,2,0:T(8,128)S(1)} %get-tuple-element.662), channel_id=1, source_target_pairs={{0,8},{8,16},{16,24},{24,32},{32,40},{40,48},{48,56},{56,64},{64,7... | collective-permute-start | bytes 294920 | tf_op jit(solution)/shard_map/ppermute | solution.py:23
  364.8 5.1 collective-permute-start.23
  367.2 5.2 collective-permute-start.22
  411.7 7.6 collective-permute-start.25
  416.9 8.6 %collective-permute-start.24 = (f32[1,16,4,3,128]{4,1,3,2,0:T(8,128)S(1)}, f32[1,16,4,3,128]{4,1,3,2,0:T(8,128)S(1)}, u32[]{:S(2)}, u32[]{:S(2)}) collective-permute-start(f32[1,16,4,3,128]{4,1,3,2,0:T(8,128)S(1)} %get-tuple-element.658), channel_id=1, source_target_pairs={{0,8},{8,16},{16,24},{24,32},{32,40},{40,48},{48,56},{56,64},{64,7... | collective-permute-start | bytes 294920 | tf_op jit(solution)/shard_map/ppermute | solution.py:23
  428.0 5.2 collective-permute-start.26
  472.5 7.6 collective-permute-start.29
  477.7 8.6 %collective-permute-start.28 = (f32[1,16,4,3,128]{4,1,3,2,0:T(8,128)S(1)}, f32[1,16,4,3,128]{4,1,3,2,0:T(8,128)S(1)}, u32[]{:S(2)}, u32[]{:S(2)}) collective-permute-start(f32[1,16,4,3,128]{4,1,3,2,0:T(8,128)S(1)} %get-tuple-element.654), channel_id=1, source_target_pairs={{0,8},{8,16},{16,24},{24,32},{32,40},{40,48},{48,56},{56,64},{64,7... | collective-permute-start | bytes 294920 | tf_op jit(solution)/shard_map/ppermute | solution.py:23
  488.8 5.2 collective-permute-start.30
  796.2 7.6 collective-permute-start.33
  801.4 8.6 %collective-permute-start.32 = (f32[1,16,4,3,128]{4,1,3,2,0:T(8,128)S(1)}, f32[1,16,4,3,128]{4,1,3,2,0:T(8,128)S(1)}, u32[]{:S(2)}, u32[]{:S(2)}) collective-permute-start(f32[1,16,4,3,128]{4,1,3,2,0:T(8,128)S(1)} %get-tuple-element.650), channel_id=1, source_target_pairs={{0,8},{8,16},{16,24},{24,32},{32,40},{40,48},{48,56},{56,64},{64,7... | collective-permute-start | bytes 294920 | tf_op jit(solution)/shard_map/ppermute | solution.py:23
  812.5 5.2 collective-permute-start.34
  (10 other events, 461.4 us)
where the time goes:
time: 833 us; the launch traced here: 823 us
  blocking collectives  299 us (36%)
  other arithmetic  135 us (16%)
  starting transfers between devices  105 us (13%)
  matrix products  93 us (11%)
  waiting for transfers between devices  76.8 us (9%)
  local copies, waits for them, and re-layouts  67.1 us (8%)
  loops' own time  44.2 us (5%)
    psum x36, blocking collectives, one_axis_at_a_time(): shard = lax.psum(shard, axis)  299 us
    another operation x128, other arithmetic  87.4 us
    ppermute x18, waiting for transfers between devices, padded_2(): lax.ppermute(tail, axis, [(i, (i + 1) % count) for i in range(ends)])  73.7 us
    ppermute x18, starting transfers between devices, padded_2(): lax.ppermute(head, axis, [((i + 1) % count, i) for i in range(ends)])  66.7 us
    another operation x1, loops' own time, solve_small(): orthonormal, triangle = lax.fori_loop(0, count, one_column, start)  43.5 us
    dot_general x32, matrix products, one_row(): total = jnp.dot(line[None, :], unknowns, precision=exact_mode)[0]  42.8 us
    ppermute x18, starting transfers between devices, padded_2(): lax.ppermute(tail, axis, [(i, (i + 1) % count) for i in range(ends)])  38 us
    dot_general x32, matrix products, one_column(): vector = vector - jnp.dot(orthonormal, second_pass, precision=exact_mode)  25.2 us
  transfers between devices with their start and end apart: 36, of which 25 were waited for; matrix products, arithmetic and copies ran while one was open for 1% of the time, Pallas kernels for 0%

commit v1 on v0

--- a/solution.py
+++ b/solution.py
@@ -31,7 +31,7 @@
 
 def one_axis_at_a_time(shard, axes):
     for axis in axes:
-        shard = lax.psum(shard, axis)
+        shard = jnp.sum(lax.all_gather(shard, axis), axis=0)
     return shard
 
 

time: 833 us -> 923 us (1.11)
  blocking collectives: 299 us -> 408 us
  starting transfers between devices: 105 us -> 94.2 us
    all_gather x0 -> x36, blocking collectives: none -> 408 us  [one_axis_at_a_time(): shard = jnp.sum(lax.all_gather(shard, axis), axis=0)]
    psum x36 -> x0, blocking collectives: 299 us -> none  [one_axis_at_a_time(): shard = lax.psum(shard, axis)]
    ppermute x18, starting transfers between devices: 66.7 us -> 48 us  [padded_2(): lax.ppermute(head, axis, [((i + 1) % count, i) for i in range(ends)])]
    ppermute x18, waiting for transfers between devices: 73.7 us -> 62.5 us  [padded_2(): lax.ppermute(tail, axis, [(i, (i + 1) % count) for i in range(ends)])]
where the time goes in v1:
time: 923 us; the launch traced here: 914 us
  blocking collectives  408 us (44%)
  other arithmetic  135 us (15%)
  starting transfers between devices  94.2 us (10%)
  matrix products  93 us (10%)
  waiting for transfers between devices  68.4 us (7%)
  local copies, waits for them, and re-layouts  67.5 us (7%)
  loops' own time  44.2 us (5%)
    all_gather x36, blocking collectives, one_axis_at_a_time(): shard = jnp.sum(lax.all_gather(shard, axis), axis=0)  408 us
    another operation x128, other arithmetic  87.4 us
    ppermute x18, waiting for transfers between devices, padded_2(): lax.ppermute(tail, axis, [(i, (i + 1) % count) for i in range(ends)])  62.5 us
    ppermute x18, starting transfers between devices, padded_2(): lax.ppermute(head, axis, [((i + 1) % count, i) for i in range(ends)])  48 us
    ppermute x18, starting transfers between devices, padded_2(): lax.ppermute(tail, axis, [(i, (i + 1) % count) for i in range(ends)])  46.2 us
    another operation x1, loops' own time, solve_small(): orthonormal, triangle = lax.fori_loop(0, count, one_column, start)  43.5 us
    dot_general x32, matrix products, one_row(): total = jnp.dot(line[None, :], unknowns, precision=exact_mode)[0]  42.8 us
    dot_general x32, matrix products, one_column(): vector = vector - jnp.dot(orthonormal, second_pass, precision=exact_mode)  25.2 us
  transfers between devices with their start and end apart: 36, of which 25 were waited for; matrix products, arithmetic and copies ran while one was open for 1% of the time, Pallas kernels for 0%

profile of v1, /device:TPU:10, one launch (start us, length us, event | category | flops | bytes accessed | tf_op | source)
XLA Modules:
  0.0 913.7 jit_solution(8915826757414846021)
XLA Ops:
  6.0 12.5 %all-gather = f32[512,4]{1,0:T(8,128)S(1)} all-gather(f32[128,4]{1,0:T(8,128)S(1)} %multiply_reduce_fusion.252), channel_id=2, replica_groups=mesh['gx_0'=4,'gx_1'=8,'gy_0'=4,'gy_1'=2] {'gx_0'}, dimensions={0}, use_global_device_ids=true | all-gather | bytes 10240 | tf_op jit(solution)/shard_map/all_gather | solution.py:34
  18.6 25.6 %all-gather.1 = f32[1024,4]{0,1:T(4,128)S(1)} all-gather(f32[128,4]{0,1:T(4,128)S(1)} %bitcast_reduce_fusion.26), channel_id=3, replica_groups=mesh['gx_0'=4,'gx_1'=8,'gy_0'=4,'gy_1'=2] {'gx_1'}, dimensions={0}, use_global_device_ids=true | all-gather | bytes 18432 | tf_op jit(solution)/shard_map/all_gather | solution.py:34
  44.2 10.9 %all-gather.2 = f32[512,4]{0,1:T(4,128)S(1)} all-gather(f32[128,4]{0,1:T(4,128)S(1)} %bitcast_reduce_fusion.8), channel_id=4, replica_groups=mesh['gx_0'=4,'gx_1'=8,'gy_0'=4,'gy_1'=2] {'gy_0'}, dimensions={0}, use_global_device_ids=true | all-gather | bytes 10240 | tf_op jit(solution)/shard_map/all_gather | solution.py:34
  82.1 12.3 %all-gather.4 = f32[512,4]{1,0:T(8,128)S(1)} all-gather(f32[128,4]{1,0:T(8,128)S(1)} %multiply_reduce_fusion.251), channel_id=6, replica_groups=mesh['gx_0'=4,'gx_1'=8,'gy_0'=4,'gy_1'=2] {'gx_0'}, dimensions={0}, use_global_device_ids=true | all-gather | bytes 10240 | tf_op jit(solution)/shard_map/all_gather | solution.py:34
  94.5 21.3 %all-gather.5 = f32[1024,4]{0,1:T(4,128)S(1)} all-gather(f32[128,4]{0,1:T(4,128)S(1)} %bitcast_reduce_fusion.24), channel_id=7, replica_groups=mesh['gx_0'=4,'gx_1'=8,'gy_0'=4,'gy_1'=2] {'gx_1'}, dimensions={0}, use_global_device_ids=true | all-gather | bytes 18432 | tf_op jit(solution)/shard_map/all_gather | solution.py:34
  115.8 10.2 %all-gather.6 = f32[512,4]{0,1:T(4,128)S(1)} all-gather(f32[128,4]{0,1:T(4,128)S(1)} %bitcast_reduce_fusion.7), channel_id=8, replica_groups=mesh['gx_0'=4,'gx_1'=8,'gy_0'=4,'gy_1'=2] {'gy_0'}, dimensions={0}, use_global_device_ids=true | all-gather | bytes 10240 | tf_op jit(solution)/shard_map/all_gather | solution.py:34
  129.1 5.4 collective-permute-start.5
  136.9 6.3 collective-permute-done.4
  156.3 11.0 %all-gather.8 = f32[512,4]{1,0:T(8,128)S(1)} all-gather(f32[128,4]{1,0:T(8,128)S(1)} %multiply_reduce_fusion.250), channel_id=10, replica_groups=mesh['gx_0'=4,'gx_1'=8,'gy_0'=4,'gy_1'=2] {'gx_0'}, dimensions={0}, use_global_device_ids=true | all-gather | bytes 10240 | tf_op jit(solution)/shard_map/all_gather | solution.py:34
  167.4 21.0 %all-gather.9 = f32[1024,4]{0,1:T(4,128)S(1)} all-gather(f32[128,4]{0,1:T(4,128)S(1)} %bitcast_reduce_fusion.22), channel_id=11, replica_groups=mesh['gx_0'=4,'gx_1'=8,'gy_0'=4,'gy_1'=2] {'gx_1'}, dimensions={0}, use_global_device_ids=true | all-gather | bytes 18432 | tf_op jit(solution)/shard_map/all_gather | solution.py:34
  188.5 10.2 %all-gather.10 = f32[512,4]{0,1:T(4,128)S(1)} all-gather(f32[128,4]{0,1:T(4,128)S(1)} %bitcast_reduce_fusion.6), channel_id=12, replica_groups=mesh['gx_0'=4,'gx_1'=8,'gy_0'=4,'gy_1'=2] {'gy_0'}, dimensions={0}, use_global_device_ids=true | all-gather | bytes 10240 | tf_op jit(solution)/shard_map/all_gather | solution.py:34
  226.2 11.7 %all-gather.12 = f32[512,4]{1,0:T(8,128)S(1)} all-gather(f32[128,4]{1,0:T(8,128)S(1)} %multiply_reduce_fusion.249), channel_id=14, replica_groups=mesh['gx_0'=4,'gx_1'=8,'gy_0'=4,'gy_1'=2] {'gx_0'}, dimensions={0}, use_global_device_ids=true | all-gather | bytes 10240 | tf_op jit(solution)/shard_map/all_gather | solution.py:34
  238.0 21.0 %all-gather.13 = f32[1024,4]{0,1:T(4,128)S(1)} all-gather(f32[128,4]{0,1:T(4,128)S(1)} %bitcast_reduce_fusion.20), channel_id=15, replica_groups=mesh['gx_0'=4,'gx_1'=8,'gy_0'=4,'gy_1'=2] {'gx_1'}, dimensions={0}, use_global_device_ids=true | all-gather | bytes 18432 | tf_op jit(solution)/shard_map/all_gather | solution.py:34
  259.1 10.2 %all-gather.14 = f32[512,4]{0,1:T(4,128)S(1)} all-gather(f32[128,4]{0,1:T(4,128)S(1)} %bitcast_reduce_fusion.5), channel_id=16, replica_groups=mesh['gx_0'=4,'gx_1'=8,'gy_0'=4,'gy_1'=2] {'gy_0'}, dimensions={0}, use_global_device_ids=true | all-gather | bytes 10240 | tf_op jit(solution)/shard_map/all_gather | solution.py:34
  297.1 11.6 %all-gather.16 = f32[512,4]{1,0:T(8,128)S(1)} all-gather(f32[128,4]{1,0:T(8,128)S(1)} %multiply_reduce_fusion.248), channel_id=18, replica_groups=mesh['gx_0'=4,'gx_1'=8,'gy_0'=4,'gy_1'=2] {'gx_0'}, dimensions={0}, use_global_device_ids=true | all-gather | bytes 10240 | tf_op jit(solution)/shard_map/all_gather | solution.py:34
  308.9 21.0 %all-gather.17 = f32[1024,4]{0,1:T(4,128)S(1)} all-gather(f32[128,4]{0,1:T(4,128)S(1)} %bitcast_reduce_fusion.18), channel_id=19, replica_groups=mesh['gx_0'=4,'gx_1'=8,'gy_0'=4,'gy_1'=2] {'gx_1'}, dimensions={0}, use_global_device_ids=true | all-gather | bytes 18432 | tf_op jit(solution)/shard_map/all_gather | solution.py:34
  329.9 10.2 %all-gather.18 = f32[512,4]{0,1:T(4,128)S(1)} all-gather(f32[128,4]{0,1:T(4,128)S(1)} %bitcast_reduce_fusion.4), channel_id=20, replica_groups=mesh['gx_0'=4,'gx_1'=8,'gy_0'=4,'gy_1'=2] {'gy_0'}, dimensions={0}, use_global_device_ids=true | all-gather | bytes 10240 | tf_op jit(solution)/shard_map/all_gather | solution.py:34
  367.8 11.8 %all-gather.20 = f32[512,4]{1,0:T(8,128)S(1)} all-gather(f32[128,4]{1,0:T(8,128)S(1)} %multiply_reduce_fusion.247), channel_id=22, replica_groups=mesh['gx_0'=4,'gx_1'=8,'gy_0'=4,'gy_1'=2] {'gx_0'}, dimensions={0}, use_global_device_ids=true | all-gather | bytes 10240 | tf_op jit(solution)/shard_map/all_gather | solution.py:34
  379.7 21.0 %all-gather.21 = f32[1024,4]{0,1:T(4,128)S(1)} all-gather(f32[128,4]{0,1:T(4,128)S(1)} %bitcast_reduce_fusion.16), channel_id=23, replica_groups=mesh['gx_0'=4,'gx_1'=8,'gy_0'=4,'gy_1'=2] {'gx_1'}, dimensions={0}, use_global_device_ids=true | all-gather | bytes 18432 | tf_op jit(solution)/shard_map/all_gather | solution.py:34
  400.7 10.2 %all-gather.22 = f32[512,4]{0,1:T(4,128)S(1)} all-gather(f32[128,4]{0,1:T(4,128)S(1)} %bitcast_reduce_fusion.3), channel_id=24, replica_groups=mesh['gx_0'=4,'gx_1'=8,'gy_0'=4,'gy_1'=2] {'gy_0'}, dimensions={0}, use_global_device_ids=true | all-gather | bytes 10240 | tf_op jit(solution)/shard_map/all_gather | solution.py:34
  420.8 5.3 collective-permute-done.20
  439.1 11.3 %all-gather.24 = f32[512,4]{1,0:T(8,128)S(1)} all-gather(f32[128,4]{1,0:T(8,128)S(1)} %multiply_reduce_fusion.246), channel_id=26, replica_groups=mesh['gx_0'=4,'gx_1'=8,'gy_0'=4,'gy_1'=2] {'gx_0'}, dimensions={0}, use_global_device_ids=true | all-gather | bytes 10240 | tf_op jit(solution)/shard_map/all_gather | solution.py:34
  450.5 21.0 %all-gather.25 = f32[1024,4]{0,1:T(4,128)S(1)} all-gather(f32[128,4]{0,1:T(4,128)S(1)} %bitcast_reduce_fusion.14), channel_id=27, replica_groups=mesh['gx_0'=4,'gx_1'=8,'gy_0'=4,'gy_1'=2] {'gx_1'}, dimensions={0}, use_global_device_ids=true | all-gather | bytes 18432 | tf_op jit(solution)/shard_map/all_gather | solution.py:34
  471.6 10.2 %all-gather.26 = f32[512,4]{0,1:T(4,128)S(1)} all-gather(f32[128,4]{0,1:T(4,128)S(1)} %bitcast_reduce_fusion.2), channel_id=28, replica_groups=mesh['gx_0'=4,'gx_1'=8,'gy_0'=4,'gy_1'=2] {'gy_0'}, dimensions={0}, use_global_device_ids=true | all-gather | bytes 10240 | tf_op jit(solution)/shard_map/all_gather | solution.py:34
  509.9 11.4 %all-gather.28 = f32[512,4]{1,0:T(8,128)S(1)} all-gather(f32[128,4]{1,0:T(8,128)S(1)} %multiply_reduce_fusion.245), channel_id=30, replica_groups=mesh['gx_0'=4,'gx_1'=8,'gy_0'=4,'gy_1'=2] {'gx_0'}, dimensions={0}, use_global_device_ids=true | all-gather | bytes 10240 | tf_op jit(solution)/shard_map/all_gather | solution.py:34
  521.4 21.0 %all-gather.29 = f32[1024,4]{0,1:T(4,128)S(1)} all-gather(f32[128,4]{0,1:T(4,128)S(1)} %bitcast_reduce_fusion.12), channel_id=31, replica_groups=mesh['gx_0'=4,'gx_1'=8,'gy_0'=4,'gy_1'=2] {'gx_1'}, dimensions={0}, use_global_device_ids=true | all-gather | bytes 18432 | tf_op jit(solution)/shard_map/all_gather | solution.py:34
  542.5 10.2 %all-gather.30 = f32[512,4]{0,1:T(4,128)S(1)} all-gather(f32[128,4]{0,1:T(4,128)S(1)} %bitcast_reduce_fusion.1), channel_id=32, replica_groups=mesh['gx_0'=4,'gx_1'=8,'gy_0'=4,'gy_1'=2] {'gy_0'}, dimensions={0}, use_global_device_ids=true | all-gather | bytes 10240 | tf_op jit(solution)/shard_map/all_gather | solution.py:34
  580.6 11.2 %all-gather.32 = f32[512,4]{1,0:T(8,128)S(1)} all-gather(f32[128,4]{1,0:T(8,128)S(1)} %multiply_reduce_fusion.244), channel_id=34, replica_groups=mesh['gx_0'=4,'gx_1'=8,'gy_0'=4,'gy_1'=2] {'gx_0'}, dimensions={0}, use_global_device_ids=true | all-gather | bytes 10240 | tf_op jit(solution)/shard_map/all_gather | solution.py:34
  591.9 21.0 %all-gather.33 = f32[1024,4]{0,1:T(4,128)S(1)} all-gather(f32[128,4]{0,1:T(4,128)S(1)} %bitcast_reduce_fusion.10), channel_id=35, replica_groups=mesh['gx_0'=4,'gx_1'=8,'gy_0'=4,'gy_1'=2] {'gx_1'}, dimensions={0}, use_global_device_ids=true | all-gather | bytes 18432 | tf_op jit(solution)/shard_map/all_gather | solution.py:34
  613.0 10.2 %all-gather.34 = f32[512,4]{0,1:T(4,128)S(1)} all-gather(f32[128,4]{0,1:T(4,128)S(1)} %bitcast_reduce_fusion), channel_id=36, replica_groups=mesh['gx_0'=4,'gx_1'=8,'gy_0'=4,'gy_1'=2] {'gy_0'}, dimensions={0}, use_global_device_ids=true | all-gather | bytes 10240 | tf_op jit(solution)/shard_map/all_gather | solution.py:34
  625.1 173.4 %while.35 = (s32[]{:T(128)}, f32[128,32]{0,1:T(8,128)S(1)}, f32[32,32]{0,1:T(8,128)S(1)}, f32[32,128]{1,0:T(8,128)S(1)}, s32[]{:T(128)}, /*index=5*/s32[1]{0:T(128)}, f32[]{:T(128)}, s32[]{:T(128)}, s32[1]{0:T(128)}) while((s32[]{:T(128)}, f32[128,32]{0,1:T(8,128)S(1)}, f32[32,32]{0,1:T(8,128)S(1)}, f32[32,128]{1,0:T(8,128)S(1)}, ...), condition=%wide.region_272.273_spmd, body=%wide.region_269.272_spmd.sunk | while | flops 197457 | bytes 72798 | solution.py:121
  798.7 85.4 %while.36 = (s32[]{:T(128)}, f32[32,4]{1,0:T(8,128)S(1)}, f32[32,4]{1,0:T(8,128)S(1)}, f32[32,32]{1,0:T(8,128)S(1)}, s32[]{:T(128)}, /*index=5*/s32[2]{0:T(128)S(1)}, s32[1]{0:T(128)}, s32[]{:T(128)}, s32[]{:T(128)}, s32[]{:T(128)}) while((s32[]{:T(128)}, f32[32,4]{1,0:T(8,128)S(1)}, f32[32,4]{1,0:T(8,128)S(1)}, ...), condition=%wide.region_275.276_spmd, body=%wide.region_273.275_spmd.sunk | while | flops 1564 | bytes 20220 | solution.py:101
  (1021 shorter events, 457.7 us)
Async XLA Ops:
  57.2 12.2 %collective-permute-start.1 = (f32[1,16,4,3,128]{4,1,3,2,0:T(8,128)S(1)}, f32[1,16,4,3,128]{4,1,3,2,0:T(8,128)S(1)}, u32[]{:S(2)}, u32[]{:S(2)}) collective-permute-start(f32[1,16,4,3,128]{4,1,3,2,0:T(8,128)S(1)} %get-tuple-element.683), channel_id=1, source_target_pairs={{8,0},{16,8},{24,16},{32,24},{40,32},{48,40},{56,48},{64,56},{72,6... | collective-permute-start | bytes 294920 | tf_op jit(solution)/shard_map/ppermute | solution.py:25
  60.5 8.9 collective-permute-start
  71.4 5.1 collective-permute-start.2
  129.1 7.8 collective-permute-start.5
  134.5 8.6 collective-permute-start.4
  143.2 4.8 collective-permute-start.7
  145.1 5.1 collective-permute-start.6
  201.8 6.8 collective-permute-start.9
  204.5 8.6 collective-permute-start.8
  215.1 5.1 collective-permute-start.10
  272.4 6.8 collective-permute-start.13
  275.4 8.6 collective-permute-start.12
  284.1 4.8 collective-permute-start.15
  286.0 5.1 collective-permute-start.14
  343.2 6.8 collective-permute-start.17
  346.1 8.6 collective-permute-start.16
  356.7 5.1 collective-permute-start.18
  414.0 6.8 collective-permute-start.21
  417.5 8.6 collective-permute-start.20
  426.1 5.0 collective-permute-start.23
  428.1 5.1 collective-permute-start.22
  484.9 6.8 collective-permute-start.25
  488.2 8.6 collective-permute-start.24
  498.8 5.1 collective-permute-start.26
  555.7 6.8 collective-permute-start.29
  559.0 8.6 collective-permute-start.28
  567.6 4.8 collective-permute-start.31
  569.6 5.1 collective-permute-start.30
  889.2 6.8 collective-permute-start.33
  892.4 8.6 collective-permute-start.32
  901.1 4.8 collective-permute-start.35
  903.0 5.1 collective-permute-start.34
  (10 other events, 524.5 us)
